TPU v7x, 32 devices: a whole 2x2x4 slice. The times are simulated.
32 devices in a mesh: gx: 8 (over y, x, core), gy: 4 (over z).
Axes of the slice: x: 2, y: 2, z: 4, core: 2. Of those that a mesh axis runs over, the one named last changes fastest.
Arguments:
- patches: bfloat16 [256, 8192], P('gy', 'gx'), may hold values from -400 to 400, as said below
- norm_gain: bfloat16 [8192], P('gx'), may hold values from 0.099609375 to 1.8984375
- gate_weight: bfloat16 [8192, 28672], P('gx', 'gy'), may hold values from -0.0625 to 0.0625
- up_weight: bfloat16 [8192, 28672], P('gx', 'gy'), may hold values from -0.0625 to 0.0625
- down_weight: bfloat16 [28672, 8192], P('gy', 'gx'), may hold values from -0.03125 to 0.03125
Outputs:
- block_out: bfloat16 [256, 8192], P('gy', 'gx')
Inputs may be any that keep to these rules, and one draw needn't show every extreme that they name: `patches`: real-valued activations of a pooled encoder.
All inputs are finite; a program needn't handle non-finite values.
Results may differ from a plain program's by a relative error of at most 0.0065.
Values may be sent and summed in bfloat16 or wider, within the bound.
No kernel may reach another device: no remote copies, remote signals or barrier semaphores. Data moves between devices by JAX's collectives and lax.ppermute only.
A program may use at most 128 MiB of HBM per device.

v0:
```python
import jax
import jax.numpy as jnp
from jax import lax
from jax.sharding import PartitionSpec as P

EPS = 1e-05


def swiglu(sums):
    return (jax.nn.silu(sums[:, 0]) * sums[:, 1]).astype(jnp.bfloat16)


def per_device(patches, norm_gain, gate_weight, up_weight, down_weight):
    values = patches.astype(jnp.float32)
    square_total = lax.psum(jnp.sum(values * values, axis=1), "gx")
    width = patches.shape[1] * lax.axis_size("gx")
    scale = lax.rsqrt(square_total / width + EPS)
    normed = (values * scale[:, None] * norm_gain.astype(jnp.float32)[None, :]).astype(jnp.bfloat16)
    whole = lax.all_gather(normed, "gy", axis=0, tiled=True)
    gate = jnp.dot(whole, gate_weight, preferred_element_type=jnp.float32)
    up = jnp.dot(whole, up_weight, preferred_element_type=jnp.float32)
    sums = lax.psum_scatter(jnp.stack([gate, up], axis=1), "gx", scatter_dimension=2, tiled=True)
    hidden = swiglu(sums)
    partial_value = jnp.dot(
        lax.all_gather(hidden, "gx", axis=1, tiled=True),
        down_weight,
        preferred_element_type=jnp.float32,
    )
    return lax.psum_scatter(partial_value, "gy", scatter_dimension=0, tiled=True).astype(
        jnp.bfloat16
    )


def solution(mesh):
    placed = (P("gy", "gx"), P("gx"), P("gx", "gy"), P("gx", "gy"), P("gy", "gx"))
    return jax.shard_map(
        per_device, mesh=mesh, in_specs=placed, out_specs=P("gy", "gx"), check_vma=False
    )
```

profile of v0, /device:TPU:0, one launch (start us, length us, event | category | flops | bytes accessed | tf_op | source)
XLA Modules:
  0.0 255.6 jit_solution(8498313657184601630)
XLA Ops:
  6.5 0.0 reduce-scatter.3.cloned.1.call-start
  6.5 1.0 fusion.2
  7.6 15.2 %psum.7 = f32[64]{0:T(128)S(1)} all-reduce(f32[64]{0:T(128)S(1)} %fusion.2), channel_id=1, replica_groups=mesh['gx'=8,'gy'=4] {'gx'}, use_global_device_ids=true, to_apply=%region_1.0 | all-reduce | flops 64 | bytes 512 | tf_op jit(solution)/shard_map/psum | solution.py:15
  22.7 0.0 copy-start
  22.7 0.8 convert_element_type.16
  23.6 1.1 fusion.4
  24.7 16.1 %all_gather.6 = bf16[256,1024]{1,0:T(8,128)(2,1)S(1)} all-gather(bf16[64,1024]{1,0:T(8,128)(2,1)S(1)} %fusion.4), channel_id=1, replica_groups=mesh['gx'=8,'gy'=4] {'gy'}, dimensions={0}, use_global_device_ids=true | all-gather | bytes 655360 | tf_op jit(solution)/shard_map/all_gather | solution.py:19
  40.8 11.2 %convolution_bitcast_fusion = f32[256,1,7168]{2,0,1:T(8,128)} fusion(bf16[256,1024]{1,0:T(8,128)(2,1)S(1)} %all_gather.6, bf16[1024,7168]{1,0:T(8,128)(2,1)} %param.8), kind=kOutput, calls=%fused_computation.1 | convolution fusion | flops 3758096384 | bytes 22544384 | tf_op jit(solution)/shard_map/dot_general | solution.py:21
  52.0 0.0 copy-done
  52.0 6.2 %convolution_bitcast_fusion.1 = f32[256,1,7168]{2,0,1:T(8,128)} fusion(bf16[256,1024]{1,0:T(8,128)(2,1)S(1)} %all_gather.6, bf16[1024,7168]{1,0:T(8,128)(2,1)S(1)} %copy-done), kind=kOutput, calls=%fused_computation.2 | convolution fusion | flops 3758096384 | bytes 22544384 | tf_op jit(solution)/shard_map/dot_general | solution.py:20
  58.2 12.1 %pad_maximum_fusion = f32[256,2,7168]{2,0,1:T(8,128)} fusion(f32[256,1,7168]{2,0,1:T(8,128)} %convolution_bitcast_fusion, f32[256,1,7168]{2,0,1:T(8,128)} %convolution_bitcast_fusion.1), kind=kLoop, calls=%fused_computation | loop fusion | flops 3670016 | bytes 29360128 | tf_op jit(solution)/shard_map/stack | solution.py:22
  70.3 0.0 reduce-scatter.3.cloned.1.call-update
  70.3 0.0 all-gather.2.cloned.1.call-start
  70.4 101.4 %reduce-scatter.3.cloned.1.call-done = f32[256,2,896]{2,0,1:T(8,128)} async-done(((f32[256,2,7168]{2,0,1:T(8,128)}), f32[256,2,896]{2,0,1:T(8,128)}) %reduce-scatter.3.cloned.1.call-update) | async-done | bytes 1835024 | tf_op jit(solution)/shard_map/reduce_scatter | solution.py:22
  171.8 2.5 fusion.1
  174.3 0.0 all-gather.2.cloned.1.call-update
  174.3 0.0 reduce-scatter.5.cloned.1.call-start
  174.4 34.4 %all-gather.2.cloned.1.call-done = bf16[256,7168]{1,0:T(8,128)(2,1)} async-done(((bf16[256,896]{1,0:T(8,128)(2,1)}), bf16[256,7168]{1,0:T(8,128)(2,1)}) %all-gather.2.cloned.1.call-update) | async-done | bytes 3670032 | tf_op jit(solution)/shard_map/all_gather | solution.py:25
  208.8 11.2 %fusion.5 = f32[256,1024]{1,0:T(8,128)} fusion(bf16[256,7168]{1,0:T(8,128)(2,1)} %all-gather.2.cloned.1.call-done, bf16[7168,1024]{1,0:T(8,128)(2,1)} %param.9), kind=kOutput, calls=%fused_computation.13 | convolution fusion | flops 3758096384 | bytes 19398656 | tf_op jit(solution)/shard_map/dot_general | solution.py:24
  220.0 0.0 reduce-scatter.5.cloned.1.call-update
  220.0 27.4 %reduce-scatter.5.cloned.1.call-done = f32[64,1024]{1,0:T(8,128)} async-done(((f32[256,1024]{1,0:T(8,128)}), f32[64,1024]{1,0:T(8,128)}) %reduce-scatter.5.cloned.1.call-update) | async-done | bytes 262160 | tf_op jit(solution)/shard_map/reduce_scatter | solution.py:29
  247.4 1.6 convert_element_type.19
  (1 shorter events, 0.0 us)
Async XLA Ops:
  6.5 165.3 %reduce-scatter.3.cloned.1.call-start = ((), (), s32[]{:S(2)}) async-start(), calls=%async_computation.2 | async-start | bytes 16515072 | tf_op jit(solution)/shard_map/reduce_scatter | solution.py:22
  22.7 29.3 %copy-start = (bf16[1024,7168]{1,0:T(8,128)(2,1)S(1)}, bf16[1024,7168]{1,0:T(8,128)(2,1)}, u32[]{:S(2)}) copy-start(bf16[1024,7168]{1,0:T(8,128)(2,1)} %param.7) | copy-start | bytes 44040196
  70.3 138.5 %all-gather.2.cloned.1.call-start = ((), (), s32[]{:S(2)}) async-start(), calls=%async_computation.3 | async-start | bytes 4128768 | tf_op jit(solution)/shard_map/all_gather | solution.py:25
  174.3 73.1 %reduce-scatter.5.cloned.1.call-start = ((), (), s32[]{:S(2)}) async-start(), calls=%async_computation.4 | async-start | bytes 1310720 | tf_op jit(solution)/shard_map/reduce_scatter | solution.py:29
Sparse Core Ops, SparseCore 0:
  70.4 101.3 reduce-scatter.2
  174.5 34.2 all-gather.1
  220.1 27.2 reduce-scatter.4
where the time goes:
time: 256 us
  waiting for transfers between devices  163 us (64%)
  blocking collectives  31.2 us (12%)
  matrix products  28.6 us (11%)
  other arithmetic  19.2 us (8%)
  between operations  13.1 us (5%)
    reduce_scatter x1, waiting for transfers between devices, per_device(): lax.psum_scatter(jnp.stack([gate, up], axis=1), 'gx', scatter_dimension=2...  101 us
    all_gather x1, waiting for transfers between devices, per_device(): lax.all_gather(hidden, 'gx', axis=1, tiled=True)  34.4 us
    reduce_scatter x1, waiting for transfers between devices, per_device(): lax.psum_scatter(partial_value, 'gy', scatter_dimension=0, tiled=True)  27.4 us
    all_gather x1, blocking collectives, per_device(): whole = lax.all_gather(normed, 'gy', axis=0, tiled=True)  16.1 us
    psum x1, blocking collectives, per_device(): square_total = lax.psum(jnp.sum(values * values, axis=1), 'gx')  15.2 us
    another operation x1, other arithmetic, per_device(): jnp.stack([gate, up], axis=1)  12.1 us
    dot_general x1, matrix products, per_device(): up = jnp.dot(whole, up_weight, preferred_element_type=jnp.float32)  11.2 us
    dot_general x1, matrix products, per_device(): jnp.dot(lax.all_gather(hidden, 'gx', axis=1, tiled=True), down_weight, pr...  11.2 us
  transfers between devices with their start and end apart: 3, of which 3 were waited for; matrix products, arithmetic and copies ran while one was open for 0% of the time, Pallas kernels for 0%

commit v1 on v0

--- a/solution.py
+++ b/solution.py
@@ -1,16 +1,22 @@
+import functools
+
 import jax
 import jax.numpy as jnp
 from jax import lax
+from jax.experimental import pallas as pl
+from jax.experimental.pallas import tpu as pltpu
 from jax.sharding import PartitionSpec as P
 
 EPS = 1e-05
+TILE = 256
+LANES = 128
 
 
 def swiglu(sums):
     return (jax.nn.silu(sums[:, 0]) * sums[:, 1]).astype(jnp.bfloat16)
 
 
-def per_device(patches, norm_gain, gate_weight, up_weight, down_weight):
+def generic(patches, norm_gain, gate_weight, up_weight, down_weight):
     values = patches.astype(jnp.float32)
     square_total = lax.psum(jnp.sum(values * values, axis=1), "gx")
     width = patches.shape[1] * lax.axis_size("gx")
@@ -31,8 +37,245 @@
     )
 
 
+def first_bit(core):
+    return 2 + 2 * core
+
+
+def second_bit(core):
+    return 4 - 2 * core
+
+
+def owner(me, p):
+    c, a, b = (p >> 2) & 1, (p >> 1) & 1, p & 1
+    core = (me & 1) ^ c
+    return me ^ c ^ (a * first_bit(core)) ^ (b * second_bit(core))
+
+
+def position(me, j):
+    c = (j ^ me) & 1
+    core = j & 1
+    diff = j ^ me ^ c
+    shift_first, shift_second = 1 + core, 2 - core
+    return c * 4 + ((diff >> shift_first) & 1) * 2 + ((diff >> shift_second) & 1)
+
+
+def swap(a, stage, n):
+    if stage == 0:
+        pairs = [(i, i ^ 1) for i in range(n)]
+    elif stage == 1:
+        pairs = [(i, i ^ first_bit(i & 1)) for i in range(n)]
+    else:
+        pairs = [(i, i ^ second_bit(i & 1)) for i in range(n)]
+    return lax.ppermute(a, "gx", pairs)
+
+
+def up_kernel(extra, nt, *refs):
+    parts, (gain, gw, uw, send, keep, lhs) = refs[:-6], refs[-6:]
+    depth, rows = len(parts), parts[0].shape[0]
+    half = rows // 2
+    j = pl.program_id(0)
+
+    @pl.when(j == 0)
+    def _():
+        for d in range(depth):
+            v = parts[d][...].astype(jnp.float32)
+            lhs[d * rows : (d + 1) * rows, :] = (v * gain[...].astype(jnp.float32)).astype(
+                jnp.bfloat16
+            )
+
+    @pl.when(j < nt)
+    def _():
+        for k, w in enumerate((gw, uw)):
+            out = jnp.dot(lhs[...], w[...], preferred_element_type=jnp.float32)
+            for d in range(depth):
+                keep[k, d] = out[d * rows : d * rows + half]
+                send[k, d] = out[d * rows + half : (d + 1) * rows].astype(jnp.bfloat16)
+
+    if extra:
+
+        @pl.when(j == nt)
+        def _():
+            for d in range(depth):
+                v = parts[d][...].astype(jnp.float32)
+                total = jnp.sum(v * v, axis=1, keepdims=True)
+                total = jnp.broadcast_to(total, (rows, TILE))
+                for k in range(2):
+                    keep[k, d] = total[:half]
+                    send[k, d] = total[half:].astype(jnp.bfloat16)
+
+
+def up_call(parts, gain, gw, uw, start, width, extra):
+    rows, feat = parts[0].shape
+    depth, half, nt = len(parts), rows // 2, width // TILE
+    cols = width + (LANES if extra else 0)
+    first = start // TILE
+    weights = pl.BlockSpec((feat, TILE), lambda j: (0, first + jnp.minimum(j, nt - 1)))
+    out = pl.BlockSpec((2, depth, half, TILE), lambda j: (0, 0, 0, j))
+    full = lambda *shape: pl.BlockSpec(shape, lambda j: (0,) * len(shape))
+    return pl.pallas_call(
+        functools.partial(up_kernel, extra, nt),
+        grid=(nt + (1 if extra else 0),),
+        in_specs=[full(rows, feat)] * depth + [full(1, feat), weights, weights],
+        out_specs=[out, out],
+        out_shape=[
+            jax.ShapeDtypeStruct((2, depth, half, cols), jnp.bfloat16),
+            jax.ShapeDtypeStruct((2, depth, half, cols), jnp.float32),
+        ],
+        scratch_shapes=[pltpu.VMEM((depth * rows, feat), jnp.bfloat16)],
+        compiler_params=pltpu.CompilerParams(
+            dimension_semantics=("arbitrary",), vmem_limit_bytes=24 << 20
+        ),
+        cost_estimate=pl.CostEstimate(
+            flops=4 * depth * rows * feat * width,
+            bytes_accessed=4 * feat * width + 12 * depth * half * width,
+            transcendentals=0,
+        ),
+        name="gate_up",
+    )(*parts, gain, gw, uw)
+
+
+def down_kernel(has_acc, last, depth, *refs):
+    pieces, refs = refs[:4], refs[4:]
+    if has_acc:
+        acc_in, refs = refs[0], refs[1:]
+    dw, refs = refs[0], refs[1:]
+    outs, (acc, lhs) = refs[:-2], refs[-2:]
+    k = pl.program_id(0)
+    sub = pieces[0].shape[1]
+    rows = 4 * sub
+
+    @pl.when(k == 0)
+    def _():
+        if has_acc:
+            acc[...] = acc_in[...]
+        else:
+            acc[...] = jnp.zeros_like(acc)
+
+    for d in range(depth):
+        for q in range(4):
+            at = d * rows + q * sub
+            lhs[at : at + sub, :] = pieces[q][d]
+    acc[...] += jnp.dot(lhs[...], dw[...], preferred_element_type=jnp.float32)
+
+    @pl.when(k == pl.num_programs(0) - 1)
+    def _():
+        if last:
+            outs[0][...] = acc[:rows]
+            for d in range(1, depth):
+                outs[d][...] = acc[d * rows : (d + 1) * rows].astype(jnp.bfloat16)
+        else:
+            outs[0][...] = acc[...]
+
+
+def down_call(pieces, acc, dw, start, last):
+    depth, sub, width = pieces[0].shape
+    feat = dw.shape[1]
+    rows = 4 * sub
+    tile = 2 * TILE if width % (2 * TILE) == 0 and start % (2 * TILE) == 0 else TILE
+    first = start // tile
+    full = lambda *shape: pl.BlockSpec(shape, lambda k: (0,) * len(shape))
+    if last:
+        shapes = [jax.ShapeDtypeStruct((rows, feat), jnp.float32)] + [
+            jax.ShapeDtypeStruct((rows, feat), jnp.bfloat16)
+        ] * (depth - 1)
+    else:
+        shapes = [jax.ShapeDtypeStruct((depth * rows, feat), jnp.float32)]
+    return pl.pallas_call(
+        functools.partial(down_kernel, acc is not None, last, depth),
+        grid=(width // tile,),
+        in_specs=[pl.BlockSpec((depth, sub, tile), lambda k: (0, 0, k))] * 4
+        + ([full(depth * rows, feat)] if acc is not None else [])
+        + [pl.BlockSpec((tile, feat), lambda k: (first + k, 0))],
+        out_specs=[full(*s.shape) for s in shapes],
+        out_shape=shapes,
+        scratch_shapes=[
+            pltpu.VMEM((depth * rows, feat), jnp.float32),
+            pltpu.VMEM((depth * rows, tile), jnp.bfloat16),
+        ],
+        compiler_params=pltpu.CompilerParams(
+            dimension_semantics=("arbitrary",), vmem_limit_bytes=24 << 20
+        ),
+        cost_estimate=pl.CostEstimate(
+            flops=2 * depth * rows * feat * width,
+            bytes_accessed=2 * feat * width + 8 * depth * rows * feat,
+            transcendentals=0,
+        ),
+        name="down",
+    )(*pieces, *([acc] if acc is not None else []), dw)
+
+
+def fast(cuts, n, m, patches, norm_gain, gate_weight, up_weight, down_weight):
+    me = lax.axis_index("gx")
+    rows, feat = patches.shape
+    sub = rows // n
+    features = feat * n
+    blocks = patches.reshape(n, sub, feat)
+    own = jnp.concatenate(
+        [lax.dynamic_slice_in_dim(blocks, owner(me, p), 1, 0) for p in range(n)], axis=0
+    ).reshape(rows, feat)
+    parts = [own] + [
+        lax.ppermute(own, "gy", [(i, i ^ d) for i in range(m)]) for d in range(1, m)
+    ]
+    gain = norm_gain.reshape(1, feat)
+
+    def received(kept, *arrived):
+        total = kept
+        for a in arrived:
+            total = total + a.astype(jnp.float32)
+        return total
+
+    start, acc, scale = 0, None, None
+    for index, width in enumerate(cuts):
+        extra = index == 0
+        send, keep = up_call(parts, gain, gate_weight, up_weight, start, width, extra)
+        r0 = swap(send, 0, n)
+        h = r0.shape[2] // 2
+        s1 = received(keep[:, :, h:], r0[:, :, h:]).astype(jnp.bfloat16)
+        r1 = swap(s1, 1, n)
+        q = h // 2
+        s2 = received(keep[:, :, q:h], r0[:, :, q:h], r1[:, :, q:]).astype(jnp.bfloat16)
+        r2 = swap(s2, 2, n)
+        sums = received(keep[:, :, :q], r0[:, :, :q], r1[:, :, :q], r2)
+        if extra:
+            scale = lax.rsqrt(sums[0, :, :, width : width + 1] / features + EPS)
+            sums = sums[:, :, :, :width]
+        gate, up = sums[0] * scale, sums[1] * scale
+        hidden = (jax.nn.silu(gate) * up).astype(jnp.bfloat16)
+        g1 = swap(hidden, 2, n)
+        near = jnp.concatenate([hidden, g1], axis=1)
+        far = swap(near, 1, n)
+        pieces = [near, far, swap(near, 0, n), swap(far, 0, n)]
+        last = index == len(cuts) - 1
+        outs = down_call(pieces, acc, down_weight, start, last)
+        acc = outs[0]
+        start += width
+    total = acc
+    for d in range(1, m):
+        total = total + lax.ppermute(outs[d], "gy", [(i, i ^ d) for i in range(m)]).astype(
+            jnp.float32
+        )
+    blocks = total.reshape(n, sub, -1)
+    return (
+        jnp.concatenate(
+            [lax.dynamic_slice_in_dim(blocks, position(me, j), 1, 0) for j in range(n)], axis=0
+        )
+        .reshape(rows, -1)
+        .astype(jnp.bfloat16)
+    )
+
+
 def solution(mesh):
+    n, m = mesh.shape["gx"], mesh.shape["gy"]
     placed = (P("gy", "gx"), P("gx"), P("gx", "gy"), P("gx", "gy"), P("gy", "gx"))
+
+    def per_device(patches, norm_gain, gate_weight, up_weight, down_weight):
+        rows, ff = patches.shape[0], gate_weight.shape[1]
+        fits = n == 8 and m in (2, 4, 8) and rows % (8 * n) == 0 and ff % (4 * TILE) == 0
+        if not fits:
+            return generic(patches, norm_gain, gate_weight, up_weight, down_weight)
+        cuts = [ff // 4] * 4
+        return fast(cuts, n, m, patches, norm_gain, gate_weight, up_weight, down_weight)
+
     return jax.shard_map(
         per_device, mesh=mesh, in_specs=placed, out_specs=P("gy", "gx"), check_vma=False
     )

time: 256 us -> 145 us (0.57)
  waiting for transfers between devices: 163 us -> 57.1 us
  Pallas kernels: 0 us -> 38 us
  starting transfers between devices: 0.09 us -> 33.4 us
  blocking collectives: 31.2 us -> 0 us
  matrix products: 28.6 us -> 0 us
  other arithmetic: 19.2 us -> 2.55 us
  between operations: 13.1 us -> 0.35 us
  local copies, waits for them, and re-layouts: 0.01 us -> 12.5 us
    reduce_scatter x2 -> x0, waiting for transfers between devices: 129 us -> none  [the longest x1 101 us: per_device(): lax.psum_scatter(jnp.stack([gate, up], axis=1), 'gx', scatter_dimension=2...]
    ppermute x0 -> x34, waiting for transfers between devices: none -> 57.1 us  [the longest x28 36.6 us: swap(): return lax.ppermute(a, 'gx', pairs)]
    pallas_call x0 -> x8, Pallas kernels: none -> 38 us  [the longest x4 28 us: up_call(): pl.pallas_call(functools.partial(up_kernel, extra, nt), grid=(nt + (1 if...]
    all_gather x1 -> x0, waiting for transfers between devices: 34.4 us -> none  [per_device(): lax.all_gather(hidden, 'gx', axis=1, tiled=True)]
    ppermute x0 -> x34, starting transfers between devices: none -> 33.4 us  [the longest x28 23.3 us: swap(): return lax.ppermute(a, 'gx', pairs)]
    dot_general x3 -> x0, matrix products: 28.6 us -> none  [the longest x1 11.2 us: per_device(): up = jnp.dot(whole, up_weight, preferred_element_type=jnp.float32)]
    all_gather x1 -> x0, blocking collectives: 16.1 us -> none  [per_device(): whole = lax.all_gather(normed, 'gy', axis=0, tiled=True)]
    psum x1 -> x0, blocking collectives: 15.2 us -> none  [per_device(): square_total = lax.psum(jnp.sum(values * values, axis=1), 'gx')]
  transfers between devices with their start and end apart: 3 -> 34, of which waited for: 3 -> 14; matrix products, arithmetic and copies ran while one was open for 0% -> 2% of each run, Pallas kernels for 0% -> 20%
where the time goes in v1:
time: 145 us; the launch traced here: 144 us
  waiting for transfers between devices  57.1 us (39%)
  Pallas kernels  38 us (26%)
  starting transfers between devices  33.4 us (23%)
  local copies, waits for them, and re-layouts  12.5 us (9%)
  other arithmetic  2.55 us (2%)
    ppermute x28, waiting for transfers between devices, swap(): return lax.ppermute(a, 'gx', pairs)  36.6 us
    pallas_call x4, Pallas kernels, up_call(): pl.pallas_call(functools.partial(up_kernel, extra, nt), grid=(nt + (1 if...  28 us
    ppermute x28, starting transfers between devices, swap(): return lax.ppermute(a, 'gx', pairs)  23.3 us
    unnamed x32, local copies, waits for them, and re-layouts  11.1 us
    ppermute x3, waiting for transfers between devices, fast(): lax.ppermute(outs[d], 'gy', [(i, i ^ d) for i in range(m)])  11 us
    pallas_call x4, Pallas kernels, down_call(): pl.pallas_call(functools.partial(down_kernel, acc is not None, last, dept...  9.97 us
    ppermute x3, waiting for transfers between devices, fast(): lax.ppermute(own, 'gy', [(i, i ^ d) for i in range(m)])  9.61 us
    ppermute x3, starting transfers between devices, fast(): lax.ppermute(own, 'gy', [(i, i ^ d) for i in range(m)])  5.64 us
  transfers between devices with their start and end apart: 34, of which 14 were waited for; matrix products, arithmetic and copies ran while one was open for 2% of the time, Pallas kernels for 20%

profile of v1, /device:TPU:0, one launch (start us, length us, event | category | flops | bytes accessed | tf_op | source)
XLA Modules:
  0.0 143.9 jit_solution(8171691079400085358)
XLA Ops:
  5.8 3.1 %collective-permute-start = (bf16[64,1024]{1,0:T(8,128)(2,1)S(1)}, bf16[64,1024]{1,0:T(8,128)(2,1)S(1)}, u32[]{:S(2)}, u32[]{:S(2)}) collective-permute-start(bf16[64,1024]{1,0:T(8,128)(2,1)S(1)} %bitcast.63), channel_id=1, source_target_pairs={{0,1},{1,0},{2,3},{3,2},{4,5},{5,4},{6,7},{7,6},{8,9},{9,8},{10,11... | collective-permute-start | bytes 393224 | tf_op jit(solution)/shard_map/ppermute | solution.py:217
  8.8 2.6 %collective-permute-start.1 = (bf16[64,1024]{1,0:T(8,128)(2,1)S(1)}, bf16[64,1024]{1,0:T(8,128)(2,1)S(1)}, u32[]{:S(2)}, u32[]{:S(2)}) collective-permute-start(bf16[64,1024]{1,0:T(8,128)(2,1)S(1)} %bitcast.64), channel_id=1, source_target_pairs={{0,2},{1,3},{2,0},{3,1},{4,6},{5,7},{6,4},{7,5},{8,10},{9,11},{10,... | collective-permute-start | bytes 393224 | tf_op jit(solution)/shard_map/ppermute | solution.py:217
  12.1 1.8 %collective-permute-done.refs_1_ = bf16[64,1024]{1,0:T(8,128)(2,1)S(1)} collective-permute-done((bf16[64,1024]{1,0:T(8,128)(2,1)S(1)}, bf16[64,1024]{1,0:T(8,128)(2,1)S(1)}, u32[]{:S(2)}, u32[]{:S(2)}) %collective-permute-start) | collective-permute-done | bytes 131104 | tf_op jit(solution)/shard_map/ppermute | solution.py:217
  13.9 7.8 %collective-permute-done.1.refs_2_ = bf16[64,1024]{1,0:T(8,128)(2,1)S(1)} collective-permute-done((bf16[64,1024]{1,0:T(8,128)(2,1)S(1)}, bf16[64,1024]{1,0:T(8,128)(2,1)S(1)}, u32[]{:S(2)}, u32[]{:S(2)}) %collective-permute-start.1) | collective-permute-done | bytes 131104 | tf_op jit(solution)/shard_map/ppermute | solution.py:217
  21.7 5.2 %copy-done = bf16[1024,7168]{1,0:T(8,128)(2,1)S(1)} copy-done((bf16[1024,7168]{1,0:T(8,128)(2,1)S(1)}, bf16[1024,7168]{1,0:T(8,128)(2,1)}, u32[]{:S(2)}) %copy-start) | copy-done | bytes 14680088
  26.9 6.5 %gate_up.4 = (bf16[2,4,32,1792]{3,2,1,0:T(8,128)(2,1)S(1)}, f32[2,4,32,1792]{3,2,1,0:T(8,128)S(1)}) custom-call(bf16[64,1024]{1,0:T(8,128)(2,1)S(1)} %bitcast.66, bf16[64,1024]{1,0:T(8,128)(2,1)S(1)} %collective-permute-done.refs_1_, bf16[64,1024]{1,0:T(8,128)(2,1)S(1)} %collective-permute-done.1.refs_2_, ...), custom_call_target="tpu_custom_call" | custom-call | flops 1879048192 | bytes 10092544 | tf_op jit(solution)/shard_map/gate_up/pallas_call | solution.py:115
  33.5 6.5 %gate_up.7 = (bf16[2,4,32,1792]{3,2,1,0:T(8,128)(2,1)S(1)}, f32[2,4,32,1792]{3,2,1,0:T(8,128)S(1)}) custom-call(bf16[64,1024]{1,0:T(8,128)(2,1)S(1)} %bitcast.67, bf16[64,1024]{1,0:T(8,128)(2,1)S(1)} %collective-permute-done.refs_1_, bf16[64,1024]{1,0:T(8,128)(2,1)S(1)} %collective-permute-done.1.refs_2_, ...), custom_call_target="tpu_custom_call" | custom-call | flops 1879048192 | bytes 10092544 | tf_op jit(solution)/shard_map/gate_up/pallas_call | solution.py:115
  40.6 7.0 %gate_up.5 = (bf16[2,4,32,1920]{3,2,1,0:T(8,128)(2,1)S(1)}, f32[2,4,32,1920]{3,2,1,0:T(8,128)S(1)}) custom-call(bf16[64,1024]{1,0:T(8,128)(2,1)S(1)} %bitcast.68, bf16[64,1024]{1,0:T(8,128)(2,1)S(1)} %collective-permute-done.refs_1_, bf16[64,1024]{1,0:T(8,128)(2,1)S(1)} %collective-permute-done.1.refs_2_, ...), custom_call_target="tpu_custom_call" | custom-call | flops 1879048192 | bytes 10092544 | tf_op jit(solution)/shard_map/gate_up/pallas_call | solution.py:115
  47.7 8.0 %gate_up.6 = (bf16[2,4,32,1792]{3,2,1,0:T(8,128)(2,1)S(1)}, f32[2,4,32,1792]{3,2,1,0:T(8,128)S(1)}) custom-call(bf16[64,1024]{1,0:T(8,128)(2,1)S(1)} %bitcast.69, bf16[64,1024]{1,0:T(8,128)(2,1)S(1)} %collective-permute-done.refs_1_, bf16[64,1024]{1,0:T(8,128)(2,1)S(1)} %collective-permute-done.1.refs_2_, ...), custom_call_target="tpu_custom_call" | custom-call | flops 1879048192 | bytes 10092544 | tf_op jit(solution)/shard_map/gate_up/pallas_call | solution.py:115
  61.0 3.9 %collective-permute-done.4 = bf16[2,4,16,1792]{3,2,1,0:T(8,128)(2,1)S(1)} collective-permute-done((bf16[2,4,16,1792]{3,2,1,0:T(8,128)(2,1)S(1)}, bf16[2,4,16,1792]{3,2,1,0:T(8,128)(2,1)S(1)}, u32[]{:S(2)}, u32[]{:S(2)}) %collective-permute-start.4) | collective-permute-done | bytes 458784 | tf_op jit(solution)/shard_map/ppermute | solution.py:69
  64.9 1.6 %collective-permute-start.5 = (bf16[2,4,8,1792]{3,2,1,0:T(8,128)(2,1)S(1)}, bf16[2,4,8,1792]{3,2,1,0:T(8,128)(2,1)S(1)}, u32[]{:S(2)}, u32[]{:S(2)}) collective-permute-start(bf16[2,4,8,1792]{3,2,1,0:T(8,128)(2,1)S(1)} %add_convert_fusion.7), channel_id=1, source_target_pairs={{0,16},{4,12},{8,24},{12,4},{16,0},{20,28},{24,8},{28,20},{1,17},{... | collective-permute-start | bytes 688136 | tf_op jit(solution)/shard_map/ppermute | solution.py:69
  66.5 5.9 %collective-permute-done.21 = bf16[2,4,16,1792]{3,2,1,0:T(8,128)(2,1)S(1)} collective-permute-done((bf16[2,4,16,1792]{3,2,1,0:T(8,128)(2,1)S(1)}, bf16[2,4,16,1792]{3,2,1,0:T(8,128)(2,1)S(1)}, u32[]{:S(2)}, u32[]{:S(2)}) %collective-permute-start.21) | collective-permute-done | bytes 458784 | tf_op jit(solution)/shard_map/ppermute | solution.py:69
  72.5 1.6 %collective-permute-start.22 = (bf16[2,4,8,1792]{3,2,1,0:T(8,128)(2,1)S(1)}, bf16[2,4,8,1792]{3,2,1,0:T(8,128)(2,1)S(1)}, u32[]{:S(2)}, u32[]{:S(2)}) collective-permute-start(bf16[2,4,8,1792]{3,2,1,0:T(8,128)(2,1)S(1)} %add_convert_fusion.5), channel_id=1, source_target_pairs={{0,16},{4,12},{8,24},{12,4},{16,0},{20,28},{24,8},{28,20},{1,17},{... | collective-permute-start | bytes 688136 | tf_op jit(solution)/shard_map/ppermute | solution.py:69
  74.1 5.9 %collective-permute-done.14 = bf16[2,4,16,1792]{3,2,1,0:T(8,128)(2,1)S(1)} collective-permute-done((bf16[2,4,16,1792]{3,2,1,0:T(8,128)(2,1)S(1)}, bf16[2,4,16,1792]{3,2,1,0:T(8,128)(2,1)S(1)}, u32[]{:S(2)}, u32[]{:S(2)}) %collective-permute-start.14) | collective-permute-done | bytes 458784 | tf_op jit(solution)/shard_map/ppermute | solution.py:69
  80.1 1.6 %collective-permute-start.15 = (bf16[2,4,8,1792]{3,2,1,0:T(8,128)(2,1)S(1)}, bf16[2,4,8,1792]{3,2,1,0:T(8,128)(2,1)S(1)}, u32[]{:S(2)}, u32[]{:S(2)}) collective-permute-start(bf16[2,4,8,1792]{3,2,1,0:T(8,128)(2,1)S(1)} %add_convert_fusion.6), channel_id=1, source_target_pairs={{0,16},{4,12},{8,24},{12,4},{16,0},{20,28},{24,8},{28,20},{1,17},{... | collective-permute-start | bytes 688136 | tf_op jit(solution)/shard_map/ppermute | solution.py:69
  81.7 5.9 %collective-permute-done.7 = bf16[2,4,16,1920]{3,2,1,0:T(8,128)(2,1)S(1)} collective-permute-done((bf16[2,4,16,1920]{3,2,1,0:T(8,128)(2,1)S(1)}, bf16[2,4,16,1920]{3,2,1,0:T(8,128)(2,1)S(1)}, u32[]{:S(2)}, u32[]{:S(2)}) %collective-permute-start.7) | collective-permute-done | bytes 491552 | tf_op jit(solution)/shard_map/ppermute | solution.py:69
  87.7 1.6 %collective-permute-start.8 = (bf16[2,4,8,1920]{3,2,1,0:T(8,128)(2,1)S(1)}, bf16[2,4,8,1920]{3,2,1,0:T(8,128)(2,1)S(1)}, u32[]{:S(2)}, u32[]{:S(2)}) collective-permute-start(bf16[2,4,8,1920]{3,2,1,0:T(8,128)(2,1)S(1)} %add_convert_fusion.4), channel_id=1, source_target_pairs={{0,16},{4,12},{8,24},{12,4},{16,0},{20,28},{24,8},{28,20},{1,17},{... | collective-permute-start | bytes 737288 | tf_op jit(solution)/shard_map/ppermute | solution.py:69
  90.5 3.4 %collective-permute-done.8 = bf16[2,4,8,1920]{3,2,1,0:T(8,128)(2,1)S(1)} collective-permute-done((bf16[2,4,8,1920]{3,2,1,0:T(8,128)(2,1)S(1)}, bf16[2,4,8,1920]{3,2,1,0:T(8,128)(2,1)S(1)}, u32[]{:S(2)}, u32[]{:S(2)}) %collective-permute-start.8) | collective-permute-done | bytes 245792 | tf_op jit(solution)/shard_map/ppermute | solution.py:69
  94.5 1.6 %collective-permute-start.9 = (bf16[4,8,1792]{2,1,0:T(8,128)(2,1)S(1)}, bf16[4,8,1792]{2,1,0:T(8,128)(2,1)S(1)}, u32[]{:S(2)}, u32[]{:S(2)}) collective-permute-start(bf16[4,8,1792]{2,1,0:T(8,128)(2,1)S(1)} %get-tuple-element.30), channel_id=1, source_target_pairs={{0,16},{4,12},{8,24},{12,4},{16,0},{20,28},{24,8},{28,20},{1,17},{... | collective-permute-start | bytes 344072 | tf_op jit(solution)/shard_map/ppermute | solution.py:69
  98.6 2.0 %collective-permute-done.9 = bf16[4,8,1792]{2,1,0:T(8,128)(2,1)S(1)} collective-permute-done((bf16[4,8,1792]{2,1,0:T(8,128)(2,1)S(1)}, bf16[4,8,1792]{2,1,0:T(8,128)(2,1)S(1)}, u32[]{:S(2)}, u32[]{:S(2)}) %collective-permute-start.9) | collective-permute-done | bytes 114720 | tf_op jit(solution)/shard_map/ppermute | solution.py:69
  100.6 1.6 %collective-permute-start.10 = (bf16[4,16,1792]{2,1,0:T(8,128)(2,1)S(1)}, bf16[4,16,1792]{2,1,0:T(8,128)(2,1)S(1)}, u32[]{:S(2)}, u32[]{:S(2)}) collective-permute-start(bf16[4,16,1792]{2,1,0:T(8,128)(2,1)S(1)} %pad_maximum_fusion.refs_0_), channel_id=1, source_target_pairs={{0,8},{4,20},{8,0},{12,28},{16,24},{20,4},{24,16},{28,12},{1,9},{5... | collective-permute-start | bytes 688136 | tf_op jit(solution)/shard_map/ppermute | solution.py:69
  102.1 3.3 %collective-permute-done.23 = bf16[4,8,1792]{2,1,0:T(8,128)(2,1)S(1)} collective-permute-done((bf16[4,8,1792]{2,1,0:T(8,128)(2,1)S(1)}, bf16[4,8,1792]{2,1,0:T(8,128)(2,1)S(1)}, u32[]{:S(2)}, u32[]{:S(2)}) %collective-permute-start.23) | collective-permute-done | bytes 114720 | tf_op jit(solution)/shard_map/ppermute | solution.py:69
  105.5 1.6 %collective-permute-start.24 = (bf16[4,16,1792]{2,1,0:T(8,128)(2,1)S(1)}, bf16[4,16,1792]{2,1,0:T(8,128)(2,1)S(1)}, u32[]{:S(2)}, u32[]{:S(2)}) collective-permute-start(bf16[4,16,1792]{2,1,0:T(8,128)(2,1)S(1)} %pad_maximum_fusion.2.refs_0_), channel_id=1, source_target_pairs={{0,8},{4,20},{8,0},{12,28},{16,24},{20,4},{24,16},{28,12},{1,9},{5... | collective-permute-start | bytes 688136 | tf_op jit(solution)/shard_map/ppermute | solution.py:69
  110.6 3.4 %collective-permute-done.28.refs_1_ = bf16[4,16,1792]{2,1,0:T(8,128)(2,1)S(1)} collective-permute-done((bf16[4,16,1792]{2,1,0:T(8,128)(2,1)S(1)}, bf16[4,16,1792]{2,1,0:T(8,128)(2,1)S(1)}, u32[]{:S(2)}, u32[]{:S(2)}) %collective-permute-start.28) | collective-permute-done | bytes 229408 | tf_op jit(solution)/shard_map/ppermute | solution.py:69
  114.6 1.9 %collective-permute-done.17.refs_1_ = bf16[4,16,1792]{2,1,0:T(8,128)(2,1)S(1)} collective-permute-done((bf16[4,16,1792]{2,1,0:T(8,128)(2,1)S(1)}, bf16[4,16,1792]{2,1,0:T(8,128)(2,1)S(1)}, u32[]{:S(2)}, u32[]{:S(2)}) %collective-permute-start.17) | collective-permute-done | bytes 229408 | tf_op jit(solution)/shard_map/ppermute | solution.py:69
  117.6 2.5 %down.4.refs_4_ = f32[256,1024]{1,0:T(8,128)S(1)} custom-call(bf16[4,16,1792]{2,1,0:T(8,128)(2,1)S(1)} %pad_maximum_fusion.3.refs_0_, bf16[4,16,1792]{2,1,0:T(8,128)(2,1)S(1)} %collective-permute-done.28.refs_1_, bf16[4,16,1792]{2,1,0:T(8,128)(2,1)S(1)} %collective-permute-done.29.refs_2_, bf16[4,16,1792]{2,1,0:T(8,128)(2,1)S(1)} %collective-permute-done.30.refs_3_, ...), custom_call_target="tpu_custom_call" | custom-call | flops 939524096 | bytes 5767168 | tf_op jit(solution)/shard_map/down/pallas_call | solution.py:183
  120.1 2.5 %down.5.refs_4_ = f32[256,1024]{1,0:T(8,128)S(1)} custom-call(bf16[4,16,1792]{2,1,0:T(8,128)(2,1)S(1)} %pad_maximum_fusion.2.refs_0_, bf16[4,16,1792]{2,1,0:T(8,128)(2,1)S(1)} %collective-permute-done.24.refs_1_, bf16[4,16,1792]{2,1,0:T(8,128)(2,1)S(1)} %collective-permute-done.25.refs_2_, bf16[4,16,1792]{2,1,0:T(8,128)(2,1)S(1)} %collective-permute-done.26.refs_3_, ...), custom_call_target="tpu_custom_call" | custom-call | flops 939524096 | bytes 5767168 | tf_op jit(solution)/shard_map/down/pallas_call | solution.py:183
  122.6 2.5 %down.6.refs_4_ = f32[256,1024]{1,0:T(8,128)S(1)} custom-call(bf16[4,16,1792]{2,1,0:T(8,128)(2,1)S(1)} %pad_maximum_fusion.1.refs_0_, bf16[4,16,1792]{2,1,0:T(8,128)(2,1)S(1)} %collective-permute-done.17.refs_1_, bf16[4,16,1792]{2,1,0:T(8,128)(2,1)S(1)} %collective-permute-done.18.refs_2_, bf16[4,16,1792]{2,1,0:T(8,128)(2,1)S(1)} %collective-permute-done.19.refs_3_, ...), custom_call_target="tpu_custom_call" | custom-call | flops 939524096 | bytes 5767168 | tf_op jit(solution)/shard_map/down/pallas_call | solution.py:183
  125.1 2.5 %down.7 = (f32[64,1024]{1,0:T(8,128)S(1)}, bf16[64,1024]{1,0:T(8,128)(2,1)S(1)}, bf16[64,1024]{1,0:T(8,128)(2,1)S(1)}, bf16[64,1024]{1,0:T(8,128)(2,1)S(1)}) custom-call(bf16[4,16,1792]{2,1,0:T(8,128)(2,1)S(1)} %pad_maximum_fusion.refs_0_, bf16[4,16,1792]{2,1,0:T(8,128)(2,1)S(1)} %collective-permute-done.10.refs_1_, ...), custom_call_target="tpu_custom_call" | custom-call | flops 939524096 | bytes 5767168 | tf_op jit(solution)/shard_map/down/pallas_call | solution.py:183
  127.6 2.3 %collective-permute-start.33 = (bf16[64,1024]{1,0:T(8,128)(2,1)S(1)}, bf16[64,1024]{1,0:T(8,128)(2,1)S(1)}, u32[]{:S(2)}, u32[]{:S(2)}) collective-permute-start(bf16[64,1024]{1,0:T(8,128)(2,1)S(1)} %get-tuple-element.28), channel_id=1, source_target_pairs={{0,3},{1,2},{2,1},{3,0},{4,7},{5,6},{6,5},{7,4},{8,11},{9,10},{10,... | collective-permute-start | bytes 393224 | tf_op jit(solution)/shard_map/ppermute | solution.py:254
  132.1 3.9 %collective-permute-done.33 = bf16[64,1024]{1,0:T(8,128)(2,1)S(1)} collective-permute-done((bf16[64,1024]{1,0:T(8,128)(2,1)S(1)}, bf16[64,1024]{1,0:T(8,128)(2,1)S(1)}, u32[]{:S(2)}, u32[]{:S(2)}) %collective-permute-start.33) | collective-permute-done | bytes 131104 | tf_op jit(solution)/shard_map/ppermute | solution.py:254
  135.9 7.1 %collective-permute-done.32 = bf16[64,1024]{1,0:T(8,128)(2,1)S(1)} collective-permute-done((bf16[64,1024]{1,0:T(8,128)(2,1)S(1)}, bf16[64,1024]{1,0:T(8,128)(2,1)S(1)}, u32[]{:S(2)}, u32[]{:S(2)}) %collective-permute-start.32) | collective-permute-done | bytes 131104 | tf_op jit(solution)/shard_map/ppermute | solution.py:254
  (99 shorter events, 25.1 us)
Async XLA Ops:
  5.8 8.1 %collective-permute-start = (bf16[64,1024]{1,0:T(8,128)(2,1)S(1)}, bf16[64,1024]{1,0:T(8,128)(2,1)S(1)}, u32[]{:S(2)}, u32[]{:S(2)}) collective-permute-start(bf16[64,1024]{1,0:T(8,128)(2,1)S(1)} %bitcast.63), channel_id=1, source_target_pairs={{0,1},{1,0},{2,3},{3,2},{4,5},{5,4},{6,7},{7,6},{8,9},{9,8},{10,11... | collective-permute-start | bytes 393224 | tf_op jit(solution)/shard_map/ppermute | solution.py:217
  8.8 12.9 %collective-permute-start.1 = (bf16[64,1024]{1,0:T(8,128)(2,1)S(1)}, bf16[64,1024]{1,0:T(8,128)(2,1)S(1)}, u32[]{:S(2)}, u32[]{:S(2)}) collective-permute-start(bf16[64,1024]{1,0:T(8,128)(2,1)S(1)} %bitcast.64), channel_id=1, source_target_pairs={{0,2},{1,3},{2,0},{3,1},{4,6},{5,7},{6,4},{7,5},{8,10},{9,11},{10,... | collective-permute-start | bytes 393224 | tf_op jit(solution)/shard_map/ppermute | solution.py:217
  11.4 10.3 %collective-permute-start.2 = (bf16[64,1024]{1,0:T(8,128)(2,1)S(1)}, bf16[64,1024]{1,0:T(8,128)(2,1)S(1)}, u32[]{:S(2)}, u32[]{:S(2)}) collective-permute-start(bf16[64,1024]{1,0:T(8,128)(2,1)S(1)} %bitcast.65), channel_id=1, source_target_pairs={{0,3},{1,2},{2,1},{3,0},{4,7},{5,6},{6,5},{7,4},{8,11},{9,10},{10,... | collective-permute-start | bytes 393224 | tf_op jit(solution)/shard_map/ppermute | solution.py:217
  33.4 22.8 %collective-permute-start.3 = (bf16[2,4,32,1792]{3,2,1,0:T(8,128)(2,1)S(1)}, bf16[2,4,32,1792]{3,2,1,0:T(8,128)(2,1)S(1)}, u32[]{:S(2)}, u32[]{:S(2)}) collective-permute-start(bf16[2,4,32,1792]{3,2,1,0:T(8,128)(2,1)S(1)} %get-tuple-element.18), channel_id=1, source_target_pairs={{0,4},{4,0},{8,12},{12,8},{16,20},{20,16},{24,28},{28,24},{1,5},{5... | collective-permute-start | bytes 2752520 | tf_op jit(solution)/shard_map/ppermute | solution.py:69
  40.0 17.8 %collective-permute-start.20 = (bf16[2,4,32,1792]{3,2,1,0:T(8,128)(2,1)S(1)}, bf16[2,4,32,1792]{3,2,1,0:T(8,128)(2,1)S(1)}, u32[]{:S(2)}, u32[]{:S(2)}) collective-permute-start(bf16[2,4,32,1792]{3,2,1,0:T(8,128)(2,1)S(1)} %get-tuple-element.24), channel_id=1, source_target_pairs={{0,4},{4,0},{8,12},{12,8},{16,20},{20,16},{24,28},{28,24},{1,5},{5... | collective-permute-start | bytes 2752520 | tf_op jit(solution)/shard_map/ppermute | solution.py:69
  47.6 12.7 %collective-permute-start.6 = (bf16[2,4,32,1920]{3,2,1,0:T(8,128)(2,1)S(1)}, bf16[2,4,32,1920]{3,2,1,0:T(8,128)(2,1)S(1)}, u32[]{:S(2)}, u32[]{:S(2)}) collective-permute-start(bf16[2,4,32,1920]{3,2,1,0:T(8,128)(2,1)S(1)} %get-tuple-element.20), channel_id=1, source_target_pairs={{0,4},{4,0},{8,12},{12,8},{16,20},{20,16},{24,28},{28,24},{1,5},{5... | collective-permute-start | bytes 2949128 | tf_op jit(solution)/shard_map/ppermute | solution.py:69
  56.3 8.5 %collective-permute-start.4 = (bf16[2,4,16,1792]{3,2,1,0:T(8,128)(2,1)S(1)}, bf16[2,4,16,1792]{3,2,1,0:T(8,128)(2,1)S(1)}, u32[]{:S(2)}, u32[]{:S(2)}) collective-permute-start(bf16[2,4,16,1792]{3,2,1,0:T(8,128)(2,1)S(1)} %add_convert_fusion.3), channel_id=1, source_target_pairs={{0,8},{4,20},{8,0},{12,28},{16,24},{20,4},{24,16},{28,12},{1,9},{5... | collective-permute-start | bytes 1376264 | tf_op jit(solution)/shard_map/ppermute | solution.py:69
  58.0 14.5 %collective-permute-start.21 = (bf16[2,4,16,1792]{3,2,1,0:T(8,128)(2,1)S(1)}, bf16[2,4,16,1792]{3,2,1,0:T(8,128)(2,1)S(1)}, u32[]{:S(2)}, u32[]{:S(2)}) collective-permute-start(bf16[2,4,16,1792]{3,2,1,0:T(8,128)(2,1)S(1)} %add_convert_fusion.1), channel_id=1, source_target_pairs={{0,8},{4,20},{8,0},{12,28},{16,24},{20,4},{24,16},{28,12},{1,9},{5... | collective-permute-start | bytes 1376264 | tf_op jit(solution)/shard_map/ppermute | solution.py:69
  58.8 21.2 %collective-permute-start.14 = (bf16[2,4,16,1792]{3,2,1,0:T(8,128)(2,1)S(1)}, bf16[2,4,16,1792]{3,2,1,0:T(8,128)(2,1)S(1)}, u32[]{:S(2)}, u32[]{:S(2)}) collective-permute-start(bf16[2,4,16,1792]{3,2,1,0:T(8,128)(2,1)S(1)} %add_convert_fusion.2), channel_id=1, source_target_pairs={{0,8},{4,20},{8,0},{12,28},{16,24},{20,4},{24,16},{28,12},{1,9},{5... | collective-permute-start | bytes 1376264 | tf_op jit(solution)/shard_map/ppermute | solution.py:69
  60.3 27.3 %collective-permute-start.7 = (bf16[2,4,16,1920]{3,2,1,0:T(8,128)(2,1)S(1)}, bf16[2,4,16,1920]{3,2,1,0:T(8,128)(2,1)S(1)}, u32[]{:S(2)}, u32[]{:S(2)}) collective-permute-start(bf16[2,4,16,1920]{3,2,1,0:T(8,128)(2,1)S(1)} %add_convert_fusion), channel_id=1, source_target_pairs={{0,8},{4,20},{8,0},{12,28},{16,24},{20,4},{24,16},{28,12},{1,9},{5... | collective-permute-start | bytes 1474568 | tf_op jit(solution)/shard_map/ppermute | solution.py:69
  64.9 24.3 %collective-permute-start.5 = (bf16[2,4,8,1792]{3,2,1,0:T(8,128)(2,1)S(1)}, bf16[2,4,8,1792]{3,2,1,0:T(8,128)(2,1)S(1)}, u32[]{:S(2)}, u32[]{:S(2)}) collective-permute-start(bf16[2,4,8,1792]{3,2,1,0:T(8,128)(2,1)S(1)} %add_convert_fusion.7), channel_id=1, source_target_pairs={{0,16},{4,12},{8,24},{12,4},{16,0},{20,28},{24,8},{28,20},{1,17},{... | collective-permute-start | bytes 688136 | tf_op jit(solution)/shard_map/ppermute | solution.py:69
  72.5 17.8 %collective-permute-start.22 = (bf16[2,4,8,1792]{3,2,1,0:T(8,128)(2,1)S(1)}, bf16[2,4,8,1792]{3,2,1,0:T(8,128)(2,1)S(1)}, u32[]{:S(2)}, u32[]{:S(2)}) collective-permute-start(bf16[2,4,8,1792]{3,2,1,0:T(8,128)(2,1)S(1)} %add_convert_fusion.5), channel_id=1, source_target_pairs={{0,16},{4,12},{8,24},{12,4},{16,0},{20,28},{24,8},{28,20},{1,17},{... | collective-permute-start | bytes 688136 | tf_op jit(solution)/shard_map/ppermute | solution.py:69
  80.1 10.3 %collective-permute-start.15 = (bf16[2,4,8,1792]{3,2,1,0:T(8,128)(2,1)S(1)}, bf16[2,4,8,1792]{3,2,1,0:T(8,128)(2,1)S(1)}, u32[]{:S(2)}, u32[]{:S(2)}) collective-permute-start(bf16[2,4,8,1792]{3,2,1,0:T(8,128)(2,1)S(1)} %add_convert_fusion.6), channel_id=1, source_target_pairs={{0,16},{4,12},{8,24},{12,4},{16,0},{20,28},{24,8},{28,20},{1,17},{... | collective-permute-start | bytes 688136 | tf_op jit(solution)/shard_map/ppermute | solution.py:69
  87.7 6.3 %collective-permute-start.8 = (bf16[2,4,8,1920]{3,2,1,0:T(8,128)(2,1)S(1)}, bf16[2,4,8,1920]{3,2,1,0:T(8,128)(2,1)S(1)}, u32[]{:S(2)}, u32[]{:S(2)}) collective-permute-start(bf16[2,4,8,1920]{3,2,1,0:T(8,128)(2,1)S(1)} %add_convert_fusion.4), channel_id=1, source_target_pairs={{0,16},{4,12},{8,24},{12,4},{16,0},{20,28},{24,8},{28,20},{1,17},{... | collective-permute-start | bytes 737288 | tf_op jit(solution)/shard_map/ppermute | solution.py:69
  94.5 6.1 %collective-permute-start.9 = (bf16[4,8,1792]{2,1,0:T(8,128)(2,1)S(1)}, bf16[4,8,1792]{2,1,0:T(8,128)(2,1)S(1)}, u32[]{:S(2)}, u32[]{:S(2)}) collective-permute-start(bf16[4,8,1792]{2,1,0:T(8,128)(2,1)S(1)} %get-tuple-element.30), channel_id=1, source_target_pairs={{0,16},{4,12},{8,24},{12,4},{16,0},{20,28},{24,8},{28,20},{1,17},{... | collective-permute-start | bytes 344072 | tf_op jit(solution)/shard_map/ppermute | solution.py:69
  96.1 13.5 %collective-permute-start.16 = (bf16[4,8,1792]{2,1,0:T(8,128)(2,1)S(1)}, bf16[4,8,1792]{2,1,0:T(8,128)(2,1)S(1)}, u32[]{:S(2)}, u32[]{:S(2)}) collective-permute-start(bf16[4,8,1792]{2,1,0:T(8,128)(2,1)S(1)} %get-tuple-element.32), channel_id=1, source_target_pairs={{0,16},{4,12},{8,24},{12,4},{16,0},{20,28},{24,8},{28,20},{1,17},{... | collective-permute-start | bytes 344072 | tf_op jit(solution)/shard_map/ppermute | solution.py:69
  96.6 8.9 %collective-permute-start.23 = (bf16[4,8,1792]{2,1,0:T(8,128)(2,1)S(1)}, bf16[4,8,1792]{2,1,0:T(8,128)(2,1)S(1)}, u32[]{:S(2)}, u32[]{:S(2)}) collective-permute-start(bf16[4,8,1792]{2,1,0:T(8,128)(2,1)S(1)} %get-tuple-element.31), channel_id=1, source_target_pairs={{0,16},{4,12},{8,24},{12,4},{16,0},{20,28},{24,8},{28,20},{1,17},{... | collective-permute-start | bytes 344072 | tf_op jit(solution)/shard_map/ppermute | solution.py:69
  98.1 9.8 %collective-permute-start.27 = (bf16[4,8,1792]{2,1,0:T(8,128)(2,1)S(1)}, bf16[4,8,1792]{2,1,0:T(8,128)(2,1)S(1)}, u32[]{:S(2)}, u32[]{:S(2)}) collective-permute-start(bf16[4,8,1792]{2,1,0:T(8,128)(2,1)S(1)} %get-tuple-element.29), channel_id=1, source_target_pairs={{0,16},{4,12},{8,24},{12,4},{16,0},{20,28},{24,8},{28,20},{1,17},{... | collective-permute-start | bytes 344072 | tf_op jit(solution)/shard_map/ppermute | solution.py:69
  100.6 9.6 %collective-permute-start.10 = (bf16[4,16,1792]{2,1,0:T(8,128)(2,1)S(1)}, bf16[4,16,1792]{2,1,0:T(8,128)(2,1)S(1)}, u32[]{:S(2)}, u32[]{:S(2)}) collective-permute-start(bf16[4,16,1792]{2,1,0:T(8,128)(2,1)S(1)} %pad_maximum_fusion.refs_0_), channel_id=1, source_target_pairs={{0,8},{4,20},{8,0},{12,28},{16,24},{20,4},{24,16},{28,12},{1,9},{5... | collective-permute-start | bytes 688136 | tf_op jit(solution)/shard_map/ppermute | solution.py:69
  105.5 8.6 %collective-permute-start.24 = (bf16[4,16,1792]{2,1,0:T(8,128)(2,1)S(1)}, bf16[4,16,1792]{2,1,0:T(8,128)(2,1)S(1)}, u32[]{:S(2)}, u32[]{:S(2)}) collective-permute-start(bf16[4,16,1792]{2,1,0:T(8,128)(2,1)S(1)} %pad_maximum_fusion.2.refs_0_), channel_id=1, source_target_pairs={{0,8},{4,20},{8,0},{12,28},{16,24},{20,4},{24,16},{28,12},{1,9},{5... | collective-permute-start | bytes 688136 | tf_op jit(solution)/shard_map/ppermute | solution.py:69
  108.0 6.1 %collective-permute-start.28 = (bf16[4,16,1792]{2,1,0:T(8,128)(2,1)S(1)}, bf16[4,16,1792]{2,1,0:T(8,128)(2,1)S(1)}, u32[]{:S(2)}, u32[]{:S(2)}) collective-permute-start(bf16[4,16,1792]{2,1,0:T(8,128)(2,1)S(1)} %pad_maximum_fusion.3.refs_0_), channel_id=1, source_target_pairs={{0,8},{4,20},{8,0},{12,28},{16,24},{20,4},{24,16},{28,12},{1,9},{5... | collective-permute-start | bytes 688136 | tf_op jit(solution)/shard_map/ppermute | solution.py:69
  109.5 7.0 %collective-permute-start.17 = (bf16[4,16,1792]{2,1,0:T(8,128)(2,1)S(1)}, bf16[4,16,1792]{2,1,0:T(8,128)(2,1)S(1)}, u32[]{:S(2)}, u32[]{:S(2)}) collective-permute-start(bf16[4,16,1792]{2,1,0:T(8,128)(2,1)S(1)} %pad_maximum_fusion.1.refs_0_), channel_id=1, source_target_pairs={{0,8},{4,20},{8,0},{12,28},{16,24},{20,4},{24,16},{28,12},{1,9},{5... | collective-permute-start | bytes 688136 | tf_op jit(solution)/shard_map/ppermute | solution.py:69
  110.1 6.4 %collective-permute-start.25 = (bf16[4,16,1792]{2,1,0:T(8,128)(2,1)S(1)}, bf16[4,16,1792]{2,1,0:T(8,128)(2,1)S(1)}, u32[]{:S(2)}, u32[]{:S(2)}) collective-permute-start(bf16[4,16,1792]{2,1,0:T(8,128)(2,1)S(1)} %pad_maximum_fusion.2.refs_0_), channel_id=1, source_target_pairs={{0,4},{4,0},{8,12},{12,8},{16,20},{20,16},{24,28},{28,24},{1,5},{5... | collective-permute-start | bytes 688136 | tf_op jit(solution)/shard_map/ppermute | solution.py:69
  110.1 6.9 %collective-permute-start.29 = (bf16[4,16,1792]{2,1,0:T(8,128)(2,1)S(1)}, bf16[4,16,1792]{2,1,0:T(8,128)(2,1)S(1)}, u32[]{:S(2)}, u32[]{:S(2)}) collective-permute-start(bf16[4,16,1792]{2,1,0:T(8,128)(2,1)S(1)} %pad_maximum_fusion.3.refs_0_), channel_id=1, source_target_pairs={{0,4},{4,0},{8,12},{12,8},{16,20},{20,16},{24,28},{28,24},{1,5},{5... | collective-permute-start | bytes 688136 | tf_op jit(solution)/shard_map/ppermute | solution.py:69
  114.0 6.0 %collective-permute-start.26 = (bf16[4,16,1792]{2,1,0:T(8,128)(2,1)S(1)}, bf16[4,16,1792]{2,1,0:T(8,128)(2,1)S(1)}, u32[]{:S(2)}, u32[]{:S(2)}) collective-permute-start(bf16[4,16,1792]{2,1,0:T(8,128)(2,1)S(1)} %collective-permute-done.24.refs_1_), channel_id=1, source_target_pairs={{0,4},{4,0},{8,12},{12,8},{16,20},{20,16},{24,28},{28,24},{1,5},{5... | collective-permute-start | bytes 688136 | tf_op jit(solution)/shard_map/ppermute | solution.py:69
  116.5 6.1 %collective-permute-start.18 = (bf16[4,16,1792]{2,1,0:T(8,128)(2,1)S(1)}, bf16[4,16,1792]{2,1,0:T(8,128)(2,1)S(1)}, u32[]{:S(2)}, u32[]{:S(2)}) collective-permute-start(bf16[4,16,1792]{2,1,0:T(8,128)(2,1)S(1)} %pad_maximum_fusion.1.refs_0_), channel_id=1, source_target_pairs={{0,4},{4,0},{8,12},{12,8},{16,20},{20,16},{24,28},{28,24},{1,5},{5... | collective-permute-start | bytes 688136 | tf_op jit(solution)/shard_map/ppermute | solution.py:69
  116.5 6.1 %collective-permute-start.19 = (bf16[4,16,1792]{2,1,0:T(8,128)(2,1)S(1)}, bf16[4,16,1792]{2,1,0:T(8,128)(2,1)S(1)}, u32[]{:S(2)}, u32[]{:S(2)}) collective-permute-start(bf16[4,16,1792]{2,1,0:T(8,128)(2,1)S(1)} %collective-permute-done.17.refs_1_), channel_id=1, source_target_pairs={{0,4},{4,0},{8,12},{12,8},{16,20},{20,16},{24,28},{28,24},{1,5},{5... | collective-permute-start | bytes 688136 | tf_op jit(solution)/shard_map/ppermute | solution.py:69
  117.0 8.1 %collective-permute-start.11 = (bf16[4,16,1792]{2,1,0:T(8,128)(2,1)S(1)}, bf16[4,16,1792]{2,1,0:T(8,128)(2,1)S(1)}, u32[]{:S(2)}, u32[]{:S(2)}) collective-permute-start(bf16[4,16,1792]{2,1,0:T(8,128)(2,1)S(1)} %pad_maximum_fusion.refs_0_), channel_id=1, source_target_pairs={{0,4},{4,0},{8,12},{12,8},{16,20},{20,16},{24,28},{28,24},{1,5},{5... | collective-permute-start | bytes 688136 | tf_op jit(solution)/shard_map/ppermute | solution.py:69
  117.1 8.0 %collective-permute-start.12 = (bf16[4,16,1792]{2,1,0:T(8,128)(2,1)S(1)}, bf16[4,16,1792]{2,1,0:T(8,128)(2,1)S(1)}, u32[]{:S(2)}, u32[]{:S(2)}) collective-permute-start(bf16[4,16,1792]{2,1,0:T(8,128)(2,1)S(1)} %collective-permute-done.10.refs_1_), channel_id=1, source_target_pairs={{0,4},{4,0},{8,12},{12,8},{16,20},{20,16},{24,28},{28,24},{1,5},{5... | collective-permute-start | bytes 688136 | tf_op jit(solution)/shard_map/ppermute | solution.py:69
  127.6 8.3 %collective-permute-start.33 = (bf16[64,1024]{1,0:T(8,128)(2,1)S(1)}, bf16[64,1024]{1,0:T(8,128)(2,1)S(1)}, u32[]{:S(2)}, u32[]{:S(2)}) collective-permute-start(bf16[64,1024]{1,0:T(8,128)(2,1)S(1)} %get-tuple-element.28), channel_id=1, source_target_pairs={{0,3},{1,2},{2,1},{3,0},{4,7},{5,6},{6,5},{7,4},{8,11},{9,10},{10,... | collective-permute-start | bytes 393224 | tf_op jit(solution)/shard_map/ppermute | solution.py:254
  129.9 13.1 %collective-permute-start.32 = (bf16[64,1024]{1,0:T(8,128)(2,1)S(1)}, bf16[64,1024]{1,0:T(8,128)(2,1)S(1)}, u32[]{:S(2)}, u32[]{:S(2)}) collective-permute-start(bf16[64,1024]{1,0:T(8,128)(2,1)S(1)} %get-tuple-element.27), channel_id=1, source_target_pairs={{0,2},{1,3},{2,0},{3,1},{4,6},{5,7},{6,4},{7,5},{8,10},{9,11},{10,... | collective-permute-start | bytes 393224 | tf_op jit(solution)/shard_map/ppermute | solution.py:254
  131.1 11.9 %collective-permute-start.31 = (bf16[64,1024]{1,0:T(8,128)(2,1)S(1)}, bf16[64,1024]{1,0:T(8,128)(2,1)S(1)}, u32[]{:S(2)}, u32[]{:S(2)}) collective-permute-start(bf16[64,1024]{1,0:T(8,128)(2,1)S(1)} %get-tuple-element.26), channel_id=1, source_target_pairs={{0,1},{1,0},{2,3},{3,2},{4,5},{5,4},{6,7},{7,6},{8,9},{9,8},{10,11... | collective-permute-start | bytes 393224 | tf_op jit(solution)/shard_map/ppermute | solution.py:254
  (11 other events, 295.8 us)
